TPU v7x, 32 devices: a whole 2x2x4 slice. The times are simulated.
32 devices in a mesh: slab: 8 (over z, x), gy: 4 (over y, core).
Axes of the slice: x: 2, y: 2, z: 4, core: 2. Of those that a mesh axis runs over, the one named last changes fastest.
Arguments:
- displacement: float32 [3, 32, 64, 512], P(None, None, 'slab', 'gy'), may hold values from -6 to 6
- previous: float32 [3, 32, 64, 512], P(None, None, 'slab', 'gy'), may hold values from -6 to 6
- shear_coef: float32 [32, 64, 512], P(None, 'slab', 'gy'), may hold values from 0.04 to 0.16
- bulk_coef: float32 [32, 64, 512], P(None, 'slab', 'gy'), may hold values from 0.02 to 0.16
- cell_index: int32 [32768], P(('slab', 'gy')), may hold values from 0 to 32767, as said below
- archetype_id: int32 [32768, 1], P(('slab', 'gy')), may hold values from 0 to 1023; in each aligned block of 1024 rows (0 to 1023, 1024 to 2047, ...) at most 2 rows name the same one
- transition: bfloat16 [1024, 256, 256], P(('slab', 'gy')), may hold values from -1 to 1
- forcing: float32 [1024, 3, 256], P(('slab', 'gy')), may hold values from -3 to 3
Outputs:
- final_field: float32 [3, 32, 64, 512], P(None, None, 'slab', 'gy')
- building_state: float32 [32768, 256], P(('slab', 'gy'))
Inputs may be any that keep to these rules, and one draw needn't show every extreme that they name: `cell_index`: building b's cell has x between s * 8 and s * 8 + 7, where s = (b // 1024) // 4; y is any. `archetype_id`: among the 1024 buildings of one device no archetype appears more than 2 times.
All inputs are finite; a program needn't handle non-finite values.
Results may differ from a plain program's by a relative error of at most 0.0023.
Values sent between devices are 32-bit elements; how exact they have to be, the bound alone decides.
A program may use at most 64 MiB of HBM per device.

v0:
```python
import jax
import jax.numpy as jnp
from jax import lax
from jax.sharding import PartitionSpec as P

COUPLINGS = 4
EVERY = 5
SUB = 6
CAP = 2


FIRST = ((-2, 1.0 / 12.0), (-1, -8.0 / 12.0), (1, 8.0 / 12.0), (2, -1.0 / 12.0))
SECOND = (
    (-2, -1.0 / 12.0),
    (-1, 16.0 / 12.0),
    (0, -30.0 / 12.0),
    (1, 16.0 / 12.0),
    (2, -1.0 / 12.0),
)
COMPONENT_AXIS = (1, 2, 0)


def padded_2(cells, sides, width):
    for axis, dim in sides:
        count = lax.axis_size(axis)
        ends = count - 1
        head = lax.slice_in_dim(cells, 0, width, axis=dim)
        tail = lax.slice_in_dim(cells, cells.shape[dim] - width, cells.shape[dim], axis=dim)
        cells = jnp.concatenate(
            [
                lax.ppermute(tail, axis, [(i, (i + 1) % count) for i in range(ends)]),
                cells,
                lax.ppermute(head, axis, [((i + 1) % count, i) for i in range(ends)]),
            ],
            axis=dim,
        )
    return cells


def pad_depth(padded):
    extent = padded.shape
    below = jnp.zeros((extent[0], 2, extent[2], extent[3]), padded.dtype)
    return jnp.concatenate([padded[:, 2:0:-1], padded, below], axis=1)


def shifted(volume, offsets):
    starts = [2 + offsets[0], 2 + offsets[1], 2 + offsets[2]]
    return volume[
        starts[0] : starts[0] + volume.shape[0] - 4,
        starts[1] : starts[1] + volume.shape[1] - 4,
        starts[2] : starts[2] + volume.shape[2] - 4,
    ]


def second_along(volume, main_axis):
    summed = None
    for amount, weight in SECOND:
        offsets = [0, 0, 0]
        offsets[main_axis] = amount
        term = weight * shifted(volume, offsets)
        summed = term if summed is None else summed + term
    return summed


def mixed_along(volume, main_axis, other_axis):
    summed = None
    for amount_a, weight_a in FIRST:
        for amount_b, weight_b in FIRST:
            offsets = [0, 0, 0]
            offsets[main_axis] = amount_a
            offsets[other_axis] = amount_b
            term = weight_a * weight_b * shifted(volume, offsets)
            summed = term if summed is None else summed + term
    return summed


def accelerate(padded, shear_coef, bulk_coef):
    results = []
    for component in range(3):
        volume = padded[component]
        main_axis = COMPONENT_AXIS[component]
        seconds = [second_along(volume, axis_a) for axis_a in range(3)]
        laplacian = seconds[0] + seconds[1] + seconds[2]
        divergence = seconds[main_axis]
        for partner in range(3):
            if partner != component:
                divergence = divergence + mixed_along(
                    padded[partner], main_axis, COMPONENT_AXIS[partner]
                )
        results.append(shear_coef * laplacian + bulk_coef * divergence)
    return jnp.stack(results)


def per_device(
    displacement, previous, shear_coef, bulk_coef, cell_index, archetype_id, transition, forcing
):
    groups = lax.axis_size("slab") * lax.axis_size("gy")
    arch_local = transition.shape[0]
    width = transition.shape[1]
    slots_dev = arch_local * CAP
    count = cell_index.shape[0]
    kinds = archetype_id[:, 0]
    order = jnp.arange(count, dtype=jnp.int32)
    earlier = (kinds[:, None] == kinds[None, :]) & (order[None, :] < order[:, None])
    position = jnp.sum(earlier.astype(jnp.int32), axis=1)
    slot_index = kinds * CAP + position
    owner = kinds // arch_local
    local_slot = slot_index - owner * slots_dev

    def one_step(index, carry):
        field, former = carry
        padded = pad_depth(padded_2(field, (("slab", 2), ("gy", 3)), 2))
        return (2.0 * field - former + accelerate(padded, shear_coef, bulk_coef), field)

    fields = (displacement, previous)
    parked = jnp.zeros((groups, slots_dev, width), jnp.float32)
    for moment in range(COUPLINGS):
        fields = lax.fori_loop(0, EVERY, one_step, fields)
        surface = lax.all_gather(fields[0][:, 0], "gy", axis=2, tiled=True)
        flat = surface.reshape(3, -1)
        local_cell = cell_index - lax.axis_index("slab") * flat.shape[1]
        ground = jnp.take(flat, local_cell, axis=1)
        motion = (
            jnp.zeros((groups, 3, slots_dev), jnp.float32).at[owner, :, local_slot].set(ground.T)
        )
        pushed = lax.all_to_all(motion, ("slab", "gy"), split_axis=0, concat_axis=0, tiled=True)
        slots = parked
        advance_motion = pushed
        slots = slots.reshape(groups, arch_local, CAP, width)
        advance_motion = advance_motion.reshape(groups, 3, arch_local, CAP)
        drive = advance_motion[:, 0, :, :, None] * forcing[None, :, 0, None, :]
        drive = drive + advance_motion[:, 1, :, :, None] * forcing[None, :, 1, None, :]
        drive = drive + advance_motion[:, 2, :, :, None] * forcing[None, :, 2, None, :]
        for inner in range(SUB):
            rounded = slots.astype(jnp.bfloat16)
            slots = (
                jnp.einsum(
                    "sack,ajk->sacj", rounded, transition, preferred_element_type=jnp.float32
                )
                + drive
            )
        parked = slots.reshape(groups, slots_dev, width)
    returned = lax.all_to_all(parked, ("slab", "gy"), split_axis=0, concat_axis=0, tiled=True)
    home_state = returned.reshape(groups * slots_dev, width)[slot_index]
    return (fields[0], home_state)


def solution(mesh):
    in_specs = (
        P(None, None, "slab", "gy"),
        P(None, None, "slab", "gy"),
        P(None, "slab", "gy"),
        P(None, "slab", "gy"),
        P(("slab", "gy")),
        P(("slab", "gy"), None),
        P(("slab", "gy"), None, None),
        P(("slab", "gy"), None, None),
    )
    out_specs = (P(None, None, "slab", "gy"), P(("slab", "gy"), None))
    return jax.shard_map(
        per_device, mesh=mesh, in_specs=in_specs, out_specs=out_specs, check_vma=False
    )
```

profile of v0, /device:TPU:0, one launch (start us, length us, event | category | flops | bytes accessed | tf_op | source)
XLA Modules:
  0.0 735.3 jit_solution(10209942065069751668)
XLA Ops:
  9.4 121.3 %while.48 = (s32[]{:T(128)}, f32[3,32,8,128]{3,1,2,0:T(8,128)S(1)}, f32[3,32,8,128]{3,1,2,0:T(8,128)S(1)}, f32[32,8,128]{2,0,1:T(8,128)S(1)}, f32[32,8,128]{2,0,...) while((s32[]{:T(128)}, f32[3,32,8,128]{3,1,2,0:T(8,128)S(1)}, f32[3,32,8,128]{3,1,2,0:T(8,128)S(1)}, ...), condition=%wide.region_1.2_spmd, body=%wide.region_0.0_spmd.sunk | while | flops 10435394 | bytes 28772140 | solution.py:118
  9.4 4.9 collective-permute-start
  16.6 4.3 collective-permute-done.1
  33.4 4.4 collective-permute-start
  40.6 4.6 collective-permute-done.1
  63.4 4.3 collective-permute-done.1
  80.8 4.4 collective-permute-start
  87.3 4.3 collective-permute-done.1
  93.7 5.1 collective-permute-start.3
  111.8 4.3 collective-permute-done.1
  118.2 5.1 collective-permute-start.3
  130.7 9.3 %all-gather = f32[3,1,8,512]{3,1,2,0:T(1,128)S(1)} all-gather(f32[3,1,8,128]{3,1,2,0:T(1,128)S(1)} %slice.1830), channel_id=2, replica_groups=mesh['slab'=8,'gy'=4] {'gy'}, dimensions={3}, use_global_device_ids=true | all-gather | bytes 61440 | tf_op jit(solution)/shard_map/all_gather | solution.py:119
  140.8 17.9 %scatter_custom_fusion = f32[3,2048]{0,1:T(8,128)} fusion(s32[1024]{0:T(1024)S(1)} %get-tuple-element.337, f32[]{:T(128)} %constant.116.clone.1, f32[]{:T(128)} %constant.113.clone.4, pred[1024]{0:T(1024)(128)(4,1)S(1)} %compare_and_fusion, f32[3,4096]{0,1:T(8,128)S(1)} %bitcast.448, s32[1024]{0:T(1024)S(1)} %get-tuple-element.336), kind=kCustom, calls=%fused_computation.1377 | custom fusion | flops 3072 | bytes 2126856
  161.0 4.4 all-to-all-start
  165.4 119.7 %while.49 = (s32[]{:T(128)}, f32[3,32,8,128]{3,1,2,0:T(8,128)S(1)}, f32[3,32,8,128]{3,1,2,0:T(8,128)S(1)}, f32[32,8,128]{2,0,1:T(8,128)S(1)}, f32[32,8,128]{2,0,...) while((s32[]{:T(128)}, f32[3,32,8,128]{3,1,2,0:T(8,128)S(1)}, f32[3,32,8,128]{3,1,2,0:T(8,128)S(1)}, ...), condition=%wide.region_3.4_spmd, body=%wide.region_2.3_spmd.sunk | while | flops 10435394 | bytes 28772140 | solution.py:118
  195.3 4.6 collective-permute-done.5
  218.1 4.3 collective-permute-done.5
  241.8 4.3 collective-permute-done.5
  248.2 5.1 collective-permute-start.7
  266.3 4.3 collective-permute-done.5
  272.7 5.1 collective-permute-start.7
  285.2 121.7 %while.50 = (s32[]{:T(128)}, f32[3,32,8,128]{3,1,2,0:T(8,128)S(1)}, f32[3,32,8,128]{3,1,2,0:T(8,128)S(1)}, f32[32,8,128]{2,0,1:T(8,128)S(1)}, f32[32,8,128]{2,0,...) while((s32[]{:T(128)}, f32[3,32,8,128]{3,1,2,0:T(8,128)S(1)}, f32[3,32,8,128]{3,1,2,0:T(8,128)S(1)}, ...), condition=%wide.region_5.6_spmd, body=%wide.region_4.5_spmd.sunk | while | flops 10435394 | bytes 28772140 | solution.py:118
  285.2 4.3 collective-permute-start.8
  291.8 4.3 collective-permute-done.9
  298.2 5.1 collective-permute-start.11
  316.3 4.3 collective-permute-done.9
  322.7 5.1 collective-permute-start.11
  340.5 4.3 collective-permute-done.9
  346.9 4.8 collective-permute-start.11
  364.4 4.3 collective-permute-done.9
  370.8 4.8 collective-permute-start.11
  388.3 4.3 collective-permute-done.9
  394.7 4.8 collective-permute-start.11
  406.9 120.0 %while.51 = (s32[]{:T(128)}, f32[3,32,8,128]{3,1,2,0:T(8,128)S(1)}, f32[3,32,8,128]{3,1,2,0:T(8,128)S(1)}, f32[32,8,128]{2,0,1:T(8,128)S(1)}, f32[32,8,128]{2,0,...) while((s32[]{:T(128)}, f32[3,32,8,128]{3,1,2,0:T(8,128)S(1)}, f32[3,32,8,128]{3,1,2,0:T(8,128)S(1)}, ...), condition=%wide.region_7.8_spmd, body=%wide.region_6.7_spmd.sunk | while | flops 10435394 | bytes 28772140 | solution.py:118
  412.7 4.3 collective-permute-done.13
  419.1 4.8 collective-permute-start.15
  436.6 4.3 collective-permute-done.13
  443.0 4.8 collective-permute-start.15
  466.9 4.8 collective-permute-start.15
  490.9 4.8 collective-permute-start.15
  514.8 4.8 collective-permute-start.15
  527.0 9.3 %all-gather.1 = f32[3,1,8,512]{3,1,2,0:T(1,128)S(1)} all-gather(f32[3,1,8,128]{3,1,2,0:T(1,128)S(1)} %slice.1837), channel_id=3, replica_groups=mesh['slab'=8,'gy'=4] {'gy'}, dimensions={3}, use_global_device_ids=true | all-gather | bytes 61440 | tf_op jit(solution)/shard_map/all_gather | solution.py:119
  537.0 7.5 %scatter_custom_fusion.1 = f32[3,2048]{0,1:T(8,128)} fusion(s32[1024]{0:T(1024)} %copy-done.7, f32[]{:T(128)} %constant.116.clone.1, f32[]{:T(128)} %constant.113.clone.4, pred[1024]{0:T(1024)(128)(4,1)S(1)} %copy-done.4, f32[3,4096]{0,1:T(8,128)S(1)} %bitcast.450, s32[1024]{0:T(1024)S(1)} %copy-done.1), kind=kCustom, calls=%fused_computation.1375 | custom fusion | flops 3072 | bytes 79872
  546.8 5.5 all-gather.2
  552.9 7.6 %scatter_custom_fusion.2 = f32[3,2048]{0,1:T(8,128)} fusion(s32[1024]{0:T(1024)} %copy-done.7, f32[]{:T(128)} %constant.116.clone.1, f32[]{:T(128)} %constant.113.clone.4, pred[1024]{0:T(1024)(128)(4,1)S(1)} %copy-done.4, f32[3,4096]{0,1:T(8,128)S(1)} %bitcast.451, s32[1024]{0:T(1024)S(1)} %copy-done.1), kind=kCustom, calls=%fused_computation.1373 | custom fusion | flops 3072 | bytes 79872
  562.9 5.2 all-gather.3
  568.7 7.5 %scatter_custom_fusion.3 = f32[3,2048]{0,1:T(8,128)} fusion(s32[1024]{0:T(1024)} %copy-done.7, f32[]{:T(128)} %constant.116.clone.1, f32[]{:T(128)} %constant.113.clone.4, pred[1024]{0:T(1024)(128)(4,1)S(1)} %copy-done.4, f32[3,4096]{0,1:T(8,128)S(1)} %bitcast.449, s32[1024]{0:T(1024)S(1)} %copy-done.1), kind=kCustom, calls=%fused_computation.1371 | custom fusion | flops 3072 | bytes 79872
  583.3 6.0 fusion.670
  589.3 6.0 fusion.668
  595.3 6.0 fusion.666
  601.3 6.1 all-to-all-start.2
  608.3 6.8 fusion.664
  615.1 6.2 fusion.662
  621.3 6.0 fusion.660
  627.3 6.0 all-to-all-start.3
  634.2 6.8 fusion.658
  641.0 6.2 fusion.656
  647.2 6.0 fusion.654
  654.2 6.0 fusion.652
  660.2 6.8 fusion.650
  666.9 6.2 bitcast_add_fusion
  675.7 5.8 all-to-all-start.4
  682.5 47.7 %all-to-all-done.4 = f32[32,64,256]{2,1,0:T(8,128)S(1)} async-done(((f32[32,64,256]{2,1,0:T(8,128)}), f32[32,64,256]{2,1,0:T(8,128)S(1)}, u32[]{:S(2)}, u32[]{:S(2)}) %all-to-all-start.4) | async-done | bytes 2097184 | tf_op jit(solution)/shard_map/all_to_all | solution.py:143
  730.3 4.7 gather_fusion
  (675 shorter events, 355.3 us)
Async XLA Ops:
  9.4 7.1 collective-permute-start
  14.3 6.5 collective-permute-start.1
  33.4 7.2 collective-permute-start
  37.8 7.5 %collective-permute-start.1 = (f32[3,32,2,128]{3,1,2,0:T(8,128)S(1)}, f32[3,32,2,128]{3,1,2,0:T(8,128)S(1)}, u32[]{:S(2)}, u32[]{:S(2)}) collective-permute-start(f32[3,32,2,128]{3,1,2,0:T(8,128)S(1)} %get-tuple-element.476), channel_id=1, source_target_pairs={{4,0},{8,4},{12,8},{16,12},{20,16},{24,20},{28,24},{5,1},{9,5},{13... | collective-permute-start | bytes 294920 | tf_op jit(solution)/shard_map/while/body/eval_jaxpr/ppermute | solution.py:33
  57.8 5.6 collective-permute-start
  61.2 6.5 collective-permute-start.1
  80.8 6.6 collective-permute-start
  85.1 6.5 collective-permute-start.1
  92.1 6.7 collective-permute-start.2
  93.7 5.9 collective-permute-start.3
  106.2 5.6 collective-permute-start
  109.6 6.5 collective-permute-start.1
  116.6 6.7 collective-permute-start.2
  118.2 5.9 collective-permute-start.3
  161.0 417.5 %all-to-all-start = ((f32[32,1,192]{2,1,0:T(1,128)}), f32[32,1,192]{2,1,0:T(1,128)}, u32[]{:S(2)}, u32[]{:S(2)}) async-start(f32[32,1,192]{2,1,0:T(1,128)} %reshape.215), calls=%async_computation | async-start | bytes 65536 | tf_op jit(solution)/shard_map/all_to_all | solution.py:126
  165.5 6.0 collective-permute-start.4
  169.1 6.5 collective-permute-start.5
  188.1 7.1 collective-permute-start.4
  192.4 7.5 %collective-permute-start.5 = (f32[3,32,2,128]{3,1,2,0:T(8,128)S(1)}, f32[3,32,2,128]{3,1,2,0:T(8,128)S(1)}, u32[]{:S(2)}, u32[]{:S(2)}) collective-permute-start(f32[3,32,2,128]{3,1,2,0:T(8,128)S(1)} %get-tuple-element.488), channel_id=1, source_target_pairs={{4,0},{8,4},{12,8},{16,12},{20,16},{24,20},{28,24},{5,1},{9,5},{13... | collective-permute-start | bytes 294920 | tf_op jit(solution)/shard_map/while/body/eval_jaxpr/ppermute | solution.py:33
  215.9 6.5 collective-permute-start.5
  235.3 6.5 collective-permute-start.4
  239.6 6.5 collective-permute-start.5
  246.7 6.7 collective-permute-start.6
  248.2 5.9 collective-permute-start.7
  260.7 5.6 collective-permute-start.4
  264.1 6.5 collective-permute-start.5
  271.1 6.7 collective-permute-start.6
  272.7 5.9 collective-permute-start.7
  285.2 6.5 collective-permute-start.8
  289.6 6.5 collective-permute-start.9
  296.6 6.7 collective-permute-start.10
  298.2 5.9 collective-permute-start.11
  310.7 5.6 collective-permute-start.8
  314.1 6.5 collective-permute-start.9
  321.1 6.7 collective-permute-start.10
  322.7 5.9 collective-permute-start.11
  338.3 6.5 collective-permute-start.9
  345.3 6.5 collective-permute-start.10
  346.9 5.6 collective-permute-start.11
  362.2 6.5 collective-permute-start.9
  369.2 6.5 collective-permute-start.10
  370.8 5.6 collective-permute-start.11
  386.1 6.5 collective-permute-start.9
  393.1 6.5 collective-permute-start.10
  394.7 5.6 collective-permute-start.11
  410.5 6.5 collective-permute-start.13
  417.5 6.5 collective-permute-start.14
  419.1 5.6 collective-permute-start.15
  434.4 6.5 collective-permute-start.13
  441.4 6.5 collective-permute-start.14
  443.0 5.6 collective-permute-start.15
  458.3 6.5 collective-permute-start.13
  465.4 6.5 collective-permute-start.14
  466.9 5.6 collective-permute-start.15
  482.3 6.5 collective-permute-start.13
  489.3 6.5 collective-permute-start.14
  490.9 5.6 collective-permute-start.15
  506.2 6.5 collective-permute-start.13
  513.2 6.5 collective-permute-start.14
  514.8 5.6 collective-permute-start.15
  578.5 22.8 %all-to-all-start.1 = ((f32[32,1,192]{2,1,0:T(1,128)}), f32[32,1,192]{2,1,0:T(1,128)S(1)}, u32[]{:S(2)}, u32[]{:S(2)}) async-start(f32[32,1,192]{2,1,0:T(1,128)} %reshape.217), calls=%async_computation.1 | async-start | bytes 65536 | tf_op jit(solution)/shard_map/all_to_all | solution.py:126
  601.3 26.0 %all-to-all-start.2 = ((f32[32,1,192]{2,1,0:T(1,128)}), f32[32,1,192]{2,1,0:T(1,128)S(1)}, u32[]{:S(2)}, u32[]{:S(2)}) async-start(f32[32,1,192]{2,1,0:T(1,128)} %reshape.219), calls=%async_computation.2 | async-start | bytes 65536 | tf_op jit(solution)/shard_map/all_to_all | solution.py:126
  627.3 25.9 %all-to-all-start.3 = ((f32[32,1,192]{2,1,0:T(1,128)}), f32[32,1,192]{2,1,0:T(1,128)S(1)}, u32[]{:S(2)}, u32[]{:S(2)}) async-start(f32[32,1,192]{2,1,0:T(1,128)} %reshape.221), calls=%async_computation.3 | async-start | bytes 65536 | tf_op jit(solution)/shard_map/all_to_all | solution.py:126
  675.7 54.6 %all-to-all-start.4 = ((f32[32,64,256]{2,1,0:T(8,128)}), f32[32,64,256]{2,1,0:T(8,128)S(1)}, u32[]{:S(2)}, u32[]{:S(2)}) async-start(f32[32,64,256]{2,1,0:T(8,128)} %copy.201), calls=%async_computation.4 | async-start | bytes 4194304 | tf_op jit(solution)/shard_map/all_to_all | solution.py:143
  (29 other events, 318.5 us)
where the time goes:
time: 742 us; the launch traced here: 735 us
  starting transfers between devices  236 us (32%)
  waiting for transfers between devices  162 us (22%)
  other arithmetic  158 us (21%)
  matrix products  74.9 us (10%)
  local copies, waits for them, and re-layouts  69.8 us (9%)
  blocking collectives  29.4 us (4%)
    ppermute x40, starting transfers between devices, padded_2(): lax.ppermute(tail, axis, [(i, (i + 1) % count) for i in range(ends)])  159 us
    ppermute x40, waiting for transfers between devices, padded_2(): lax.ppermute(head, axis, [((i + 1) % count, i) for i in range(ends)])  86.2 us
    another operation x60, other arithmetic, accelerate(): return jnp.stack(results)  82.7 us
    dot_general x12, matrix products, per_device(): jnp.einsum('sack,ajk->sacj', rounded, transition, preferred_element_type=...  74.9 us
    ppermute x40, starting transfers between devices, padded_2(): lax.ppermute(head, axis, [((i + 1) % count, i) for i in range(ends)])  51.7 us
    all_to_all x1, waiting for transfers between devices, per_device(): lax.all_to_all(parked, ('slab', 'gy'), split_axis=0, concat_axis=0, tiled...  47.7 us
    unnamed x6, other arithmetic  41.9 us
    all_gather x4, blocking collectives, per_device(): surface = lax.all_gather(fields[0][:, 0], 'gy', axis=2, tiled=True)  29.4 us
  transfers between devices with their start and end apart: 85, of which 61 were waited for; matrix products, arithmetic and copies ran while one was open for 29% of the time, Pallas kernels for 0%

commit v1 on v0

v1 whole, which is shorter than its diff:
```python
import functools

import jax
import jax.numpy as jnp
from jax import lax
from jax.experimental import pallas as pl
from jax.experimental.pallas import tpu as pltpu
from jax.sharding import PartitionSpec as P

COUPLINGS = 4
EVERY = 5
SUB = 6
CAP = 2
CHUNKS = 2
ARCH_BLOCK = 4
PLANES = 4

A0, A1, A2 = -30.0 / 12.0, 16.0 / 12.0, -1.0 / 12.0
B1, B2 = 8.0 / 12.0, -1.0 / 12.0
DIRECTIONS = ((-1, 0), (1, 0), (0, -1), (0, 1), (-1, -1), (1, -1), (-1, 1), (1, 1))


def second(mid, plus1, minus1, plus2, minus2):
    return A0 * mid + A1 * (plus1 + minus1) + A2 * (plus2 + minus2)


def first(plus1, minus1, plus2, minus2):
    return B1 * (plus1 - minus1) + B2 * (plus2 - minus2)


def grid_kernel(
    steps, every, d_ref, p_ref, sh_ref, bk_ref, f_ref, surf_ref,
    buf, ps, pr, ht, ah, hx, e_ref, s_ref, send, recv,
):
    nz, cx, cy = sh_ref.shape
    slab, gy = lax.axis_index("slab"), lax.axis_index("gy")
    slabs, gys = lax.axis_size("slab"), lax.axis_size("gy")
    blocks = nz // PLANES

    def exists(dx, dy):
        x, y = slab + dx, gy + dy
        return (x >= 0) & (x < slabs) & (y >= 0) & (y < gys)

    buf[...] = jnp.zeros_like(buf)
    pr[...] = jnp.zeros_like(pr)
    ht[...] = jnp.zeros_like(ht)
    e_ref[...] = jnp.zeros_like(e_ref)
    buf[0, :, 2 : nz + 2, 8:16, :] = d_ref[...]
    buf[1, :, 2 : nz + 2, 8:16, :] = p_ref[...]

    barrier = pltpu.get_barrier_semaphore()
    for dx, dy in DIRECTIONS:
        @pl.when(exists(dx, dy))
        def _():
            pl.semaphore_signal(
                barrier, inc=1, device_id=(slab + dx, gy + dy),
                device_id_type=pl.DeviceIdType.MESH,
            )
    spans = [
        1 + jnp.where(at > 0, 1, 0) + jnp.where(at < size - 1, 1, 0)
        for at, size in ((slab, slabs), (gy, gys))
    ]
    pl.semaphore_wait(barrier, spans[0] * spans[1] - 1)

    def copy_of(k, par):
        dx, dy = DIRECTIONS[k]
        mine = slice(0, 2) if dx < 0 else slice(cx - 2, cx)
        theirs = slice(16, 18) if dx < 0 else slice(6, 8)
        if dy == 0:
            src = buf.at[par, :, 2 : nz + 2, mine.start + 8 : mine.stop + 8, :]
            dst = buf.at[par, :, 2 : nz + 2, theirs, :]
        elif dx == 0:
            src = ps.at[par]
            dst = pr.at[par, 1 if dy < 0 else 0, :, 8:16, :]
        else:
            src = ps.at[par, :, mine, :]
            dst = pr.at[par, 1 if dy < 0 else 0, :, theirs, :]
        return pltpu.make_async_remote_copy(
            src_ref=src, dst_ref=dst, send_sem=send.at[par, k], recv_sem=recv.at[par, k],
            device_id=(slab + dx, gy + dy), device_id_type=pl.DeviceIdType.MESH,
        )

    lane3 = lax.broadcasted_iota(jnp.int32, (PLANES, cx, cy), 2)
    lane = lax.broadcasted_iota(jnp.int32, (cx, cy), 1)
    row3 = lax.broadcasted_iota(jnp.int32, (PLANES, cx, cy), 1)
    row = lax.broadcasted_iota(jnp.int32, (cx, cy), 0)

    def along_y(core, halo):
        return (
            pltpu.roll(jnp.where(lane3 < 1, halo, core), cy - 1, 2),
            pltpu.roll(jnp.where(lane3 >= cy - 1, halo, core), 1, 2),
            pltpu.roll(jnp.where(lane3 < 2, halo, core), cy - 2, 2),
            pltpu.roll(jnp.where(lane3 >= cy - 2, halo, core), 2, 2),
        )

    def step(n, carry):
        par = lax.rem(n, 2)
        new = 1 - par

        for k in range(2):
            @pl.when(exists(*DIRECTIONS[k]))
            def _():
                copy_of(k, par).start()

        for c in range(3):
            packed = jnp.zeros((cx, cy), jnp.float32)
            for d in range(nz):
                turned = pltpu.roll(buf[par, c, d + 2, 8:16, :], 2 + 4 * d, 1) if (2 + 4 * d) % cy else buf[par, c, d + 2, 8:16, :]
                packed = jnp.where((lane >= 4 * d) & (lane < 4 * d + 4), turned, packed)
            ps[par, c] = packed

        for k in range(2, 8):
            @pl.when(exists(*DIRECTIONS[k]))
            def _():
                copy_of(k, par).start()

        for c in range(3):
            buf[par, c, 0, 8:16, :] = buf[par, c, 4, 8:16, :]
            buf[par, c, 1, 8:16, :] = buf[par, c, 3, 8:16, :]

        for k in range(8):
            @pl.when(exists(*DIRECTIONS[k]))
            def _():
                copy_of(k, par).wait_send()
        for k in range(8):
            dx, dy = DIRECTIONS[k]
            @pl.when(exists(-dx, -dy))
            def _():
                copy_of(k, par).wait_recv()

        for lo in (0, 16):
            buf[par, 2, 0, lo : lo + 8, :] = buf[par, 2, 4, lo : lo + 8, :]
            buf[par, 2, 1, lo : lo + 8, :] = buf[par, 2, 3, lo : lo + 8, :]

        from_left = lax.rem(lane, 4) < 2

        def joined(c, lo):
            return jnp.where(from_left, pr[par, 0, c, lo : lo + 8, :], pr[par, 1, c, lo : lo + 8, :])

        g = [joined(c, 8) for c in range(3)]
        g_y = jnp.where(row < 4, joined(1, 16), joined(1, 0))
        g_x = jnp.where(row < 4, joined(0, 16), joined(0, 0))
        a_g = first(
            pltpu.roll(jnp.where(row < 1, g_x, g[0]), cx - 1, 0),
            pltpu.roll(jnp.where(row >= cx - 1, g_x, g[0]), 1, 0),
            pltpu.roll(jnp.where(row < 2, g_x, g[0]), cx - 2, 0),
            pltpu.roll(jnp.where(row >= cx - 2, g_x, g[0]), 2, 0),
        )
        for d in range(nz):
            back = (cy - 4 * d - 2) % cy
            for c in range(3):
                ht[c, d + 2] = pltpu.roll(g[c], back, 1)
            ah[d] = pltpu.roll(a_g, back, 1)
            hx[d] = pltpu.roll(g_y, back, 1)
        ht[2, 0] = ht[2, 4]
        ht[2, 1] = ht[2, 3]

        def u(c, d, shift, lo):
            return buf[par, c, pl.ds(d + 2 + shift, PLANES), lo : lo + 8, :]

        def prepare(b, carry):
            d = b * PLANES
            a = first(u(0, d, 0, 9), u(0, d, 0, 7), u(0, d, 0, 10), u(0, d, 0, 6))
            bb = first(*along_y(u(1, d, 0, 8), ht[1, pl.ds(d + 2, PLANES)]))
            e_ref[pl.ds(d + 2, PLANES)] = a + bb
            cc = first(u(2, d, 1, 8), u(2, d, -1, 8), u(2, d, 2, 8), u(2, d, -2, 8))
            s_ref[pl.ds(d, PLANES), 8:16, :] = bb + cc

            def mixed(comp, shift):
                return jnp.where(row3 < 4, u(comp, d, shift, 16), u(comp, d, shift, 0))

            s_halo = first(*along_y(mixed(1, 0), hx[pl.ds(d, PLANES)])) + first(
                mixed(2, 1), mixed(2, -1), mixed(2, 2), mixed(2, -2)
            )
            s_ref[pl.ds(d, PLANES), 0:8, :] = s_halo
            s_ref[pl.ds(d, PLANES), 16:24, :] = s_halo
            return carry

        lax.fori_loop(0, blocks, prepare, 0)
        e_ref[0] = e_ref[4]
        e_ref[1] = e_ref[3]

        def advance(b, carry):
            d = b * PLANES
            sh = sh_ref[pl.ds(d, PLANES)]
            bk = bk_ref[pl.ds(d, PLANES)]

            def h(c, shift):
                return ht[c, pl.ds(d + 2 + shift, PLANES)]

            def s(lo):
                return s_ref[pl.ds(d, PLANES), lo : lo + 8, :]

            def e(shift):
                return e_ref[pl.ds(d + 2 + shift, PLANES)]

            a = first(u(0, d, 0, 9), u(0, d, 0, 7), u(0, d, 0, 10), u(0, d, 0, 6))
            cc = first(u(2, d, 1, 8), u(2, d, -1, 8), u(2, d, 2, 8), u(2, d, -2, 8))
            c_halo = first(h(2, 1), h(2, -1), h(2, 2), h(2, -2))
            t_halo = ah[pl.ds(d, PLANES)] + c_halo
            for c in range(3):
                mid = u(c, d, 0, 8)
                along = (
                    second(mid, u(c, d, 0, 9), u(c, d, 0, 7), u(c, d, 0, 10), u(c, d, 0, 6)),
                    second(mid, *along_y(mid, h(c, 0))),
                    second(mid, u(c, d, 1, 8), u(c, d, -1, 8), u(c, d, 2, 8), u(c, d, -2, 8)),
                )
                if c == 0:
                    cross = first(s(9), s(7), s(10), s(6))
                elif c == 1:
                    cross = first(*along_y(a + cc, t_halo))
                else:
                    cross = first(e(1), e(-1), e(2), e(-2))
                acc = sh * (along[0] + along[1] + along[2]) + bk * (along[c] + cross)
                place = (new, c, pl.ds(d + 2, PLANES), slice(8, 16), slice(None))
                buf[place] = 2.0 * mid - buf[place] + acc
            return carry

        lax.fori_loop(0, blocks, advance, 0)
        surf_ref[lax.div(n, every)] = buf[new, :, 2, 8:16, :]
        return carry

    lax.fori_loop(0, steps, step, 0)
    f_ref[...] = buf[steps % 2, :, 2 : nz + 2, 8:16, :]


def run_grid(displacement, previous, shear_coef, bulk_coef):
    _, nz, cx, cy = displacement.shape
    vmem = pl.BlockSpec(memory_space=pltpu.VMEM)
    f32 = jnp.float32
    return pl.pallas_call(
        functools.partial(grid_kernel, COUPLINGS * EVERY, EVERY),
        out_shape=(
            jax.ShapeDtypeStruct(displacement.shape, f32),
            jax.ShapeDtypeStruct((COUPLINGS, 3, cx, cy), f32),
        ),
        in_specs=[vmem] * 4,
        out_specs=(vmem, vmem),
        scratch_shapes=[
            pltpu.VMEM((2, 3, nz + 4, cx + 16, cy), f32),
            pltpu.VMEM((2, 3, cx, cy), f32),
            pltpu.VMEM((2, 2, 3, cx + 16, cy), f32),
            pltpu.VMEM((3, nz + 4, cx, cy), f32),
            pltpu.VMEM((nz, cx, cy), f32),
            pltpu.VMEM((nz, cx, cy), f32),
            pltpu.VMEM((nz + 4, cx, cy), f32),
            pltpu.VMEM((nz, cx + 16, cy), f32),
            pltpu.SemaphoreType.DMA((2, 8)),
            pltpu.SemaphoreType.DMA((2, 8)),
        ],
        compiler_params=pltpu.CompilerParams(
            collective_id=0, has_side_effects=True, vmem_limit_bytes=32 * 1024 * 1024
        ),
    )(displacement, previous, shear_coef, bulk_coef)


def building_kernel(couplings, sub, m_ref, f_ref, t_ref, o_ref):
    block, rows, _ = m_ref.shape
    width = t_ref.shape[1]
    states = [jnp.zeros((rows, width), jnp.float32) for _ in range(block)]
    for moment in range(couplings):
        drives = []
        for i in range(block):
            drive = m_ref[i, :, 3 * moment : 3 * moment + 1] * f_ref[i, 0:1, :]
            drive = drive + m_ref[i, :, 3 * moment + 1 : 3 * moment + 2] * f_ref[i, 1:2, :]
            drive = drive + m_ref[i, :, 3 * moment + 2 : 3 * moment + 3] * f_ref[i, 2:3, :]
            drives.append(drive)
        for inner in range(sub):
            for i in range(block):
                if moment == 0 and inner == 0:
                    states[i] = drives[i]
                else:
                    states[i] = drives[i] + lax.dot_general(
                        states[i].astype(jnp.bfloat16), t_ref[i],
                        (((1,), (1,)), ((), ())), preferred_element_type=jnp.float32,
                    )
    for i in range(block):
        o_ref[:, CAP * i : CAP * (i + 1), :] = states[i].reshape(rows // CAP, CAP, width)


def run_buildings(motion, forcing, transition, start, kinds):
    rows, parts = motion.shape[1], motion.shape[2]
    width = transition.shape[1]
    first_block = start // ARCH_BLOCK
    return pl.pallas_call(
        functools.partial(building_kernel, COUPLINGS, SUB),
        grid=(kinds // ARCH_BLOCK,),
        out_shape=jax.ShapeDtypeStruct((rows // CAP, kinds * CAP, width), jnp.float32),
        in_specs=[
            pl.BlockSpec((ARCH_BLOCK, rows, parts), lambda i: (i + first_block, 0, 0)),
            pl.BlockSpec((ARCH_BLOCK, 3, width), lambda i: (i + first_block, 0, 0)),
            pl.BlockSpec((ARCH_BLOCK, width, width), lambda i: (i + first_block, 0, 0)),
        ],
        out_specs=pl.BlockSpec((rows // CAP, ARCH_BLOCK * CAP, width), lambda i: (0, i, 0)),
        cost_estimate=pl.CostEstimate(
            flops=2 * kinds * rows * width * width * COUPLINGS * SUB,
            bytes_accessed=2 * kinds * width * width + 4 * kinds * rows * width,
            transcendentals=0,
        ),
    )(motion, forcing, transition)


def per_device(
    displacement, previous, shear_coef, bulk_coef, cell_index, archetype_id, transition, forcing
):
    groups = lax.axis_size("slab") * lax.axis_size("gy")
    arch_local = transition.shape[0]
    width = transition.shape[1]
    slots_dev = arch_local * CAP
    count = cell_index.shape[0]
    kinds = archetype_id[:, 0]
    order = jnp.arange(count, dtype=jnp.int32)
    earlier = (kinds[:, None] == kinds[None, :]) & (order[None, :] < order[:, None])
    position = jnp.sum(earlier.astype(jnp.int32), axis=1)
    slot_index = kinds * CAP + position
    cells = displacement.shape[2] * displacement.shape[3] * lax.axis_size("gy")
    local_cell = cell_index - lax.axis_index("slab") * cells
    slots = jnp.arange(groups * slots_dev, dtype=jnp.int32)
    slot_cell = jnp.sum(
        jnp.where(slot_index[None, :] == slots[:, None], local_cell[None, :], 0), axis=1
    )

    field, surface = run_grid(displacement, previous, shear_coef, bulk_coef)

    parts = 3 * COUPLINGS
    surface = lax.all_gather(surface, "gy", axis=3, tiled=True)
    table = surface.reshape(parts, cells).T
    motion = jnp.take(table, slot_cell, axis=0, mode="clip")
    motion = motion.reshape(groups, slots_dev, parts).transpose(0, 2, 1)
    pushed = lax.all_to_all(motion, ("slab", "gy"), split_axis=0, concat_axis=0, tiled=True)
    pushed = pushed.reshape(groups, parts, arch_local, CAP).transpose(2, 0, 3, 1)
    pushed = pushed.reshape(arch_local, groups * CAP, parts)

    share = arch_local // CHUNKS
    pieces = []
    for chunk in range(CHUNKS):
        states = run_buildings(pushed, forcing, transition, chunk * share, share)
        returned = lax.all_to_all(
            states, ("slab", "gy"), split_axis=0, concat_axis=0, tiled=True
        )
        pieces.append(returned.reshape(groups * share * CAP, width))
    owner, kind = kinds // arch_local, kinds % arch_local
    chunk_of = kind // share
    home = chunk_of * (groups * share * CAP) + owner * (share * CAP)
    home = home + (kind - chunk_of * share) * CAP + position
    home_state = jnp.take(jnp.concatenate(pieces, axis=0), home, axis=0, mode="clip")
    return (field, home_state)


def solution(mesh):
    in_specs = (
        P(None, None, "slab", "gy"),
        P(None, None, "slab", "gy"),
        P(None, "slab", "gy"),
        P(None, "slab", "gy"),
        P(("slab", "gy")),
        P(("slab", "gy"), None),
        P(("slab", "gy"), None, None),
        P(("slab", "gy"), None, None),
    )
    out_specs = (P(None, None, "slab", "gy"), P(("slab", "gy"), None))
    return jax.shard_map(
        per_device, mesh=mesh, in_specs=in_specs, out_specs=out_specs, check_vma=False
    )
```

time: 742 us -> 309 us (0.42)
  starting transfers between devices: 236 us -> 12.9 us
  Pallas kernels: 0 us -> 220 us
  other arithmetic: 158 us -> 5.23 us
  waiting for transfers between devices: 162 us -> 41.6 us
  matrix products: 74.9 us -> 0 us
  local copies, waits for them, and re-layouts: 69.8 us -> 21.5 us
  blocking collectives: 29.4 us -> 5.6 us
    pallas_call x0 -> x3, Pallas kernels: none -> 220 us  [the longest x1 187 us: run_grid(): pl.pallas_call(functools.partial(grid_kernel, COUPLINGS * EVERY, EVERY),...]
    ppermute x80 -> x0, starting transfers between devices: 211 us -> none  [the longest x40 159 us: padded_2(): lax.ppermute(tail, axis, [(i, (i + 1) % count) for i in range(ends)])]
    ppermute x80 -> x0, waiting for transfers between devices: 115 us -> none  [the longest x40 86.2 us: padded_2(): lax.ppermute(head, axis, [((i + 1) % count, i) for i in range(ends)])]
    another operation x60 -> x0, other arithmetic: 82.7 us -> none  [accelerate(): return jnp.stack(results)]
    dot_general x12 -> x0, matrix products: 74.9 us -> none  [per_device(): jnp.einsum('sack,ajk->sacj', rounded, transition, preferred_element_type=...]
    unnamed x6 -> x0, other arithmetic: 41.9 us -> none
    all_gather x4 -> x1, blocking collectives: 29.4 us -> 5.6 us  [per_device(): surface = lax.all_gather(surface, 'gy', axis=3, tiled=True)]
    while x104 -> x0, local copies, waits for them, and re-layouts: 16.6 us -> none
  transfers between devices with their start and end apart: 85 -> 3, of which waited for: 61 -> 3; matrix products, arithmetic and copies ran while one was open for 29% -> 1% of each run, Pallas kernels for 0% -> 5%
where the time goes in v1:
time: 309 us; the launch traced here: 308 us
  Pallas kernels  220 us (71%)
  waiting for transfers between devices  41.6 us (13%)
  local copies, waits for them, and re-layouts  21.5 us (7%)
  starting transfers between devices  12.9 us (4%)
  blocking collectives  5.6 us (2%)
  other arithmetic  5.23 us (2%)
    pallas_call x1, Pallas kernels, run_grid(): pl.pallas_call(functools.partial(grid_kernel, COUPLINGS * EVERY, EVERY),...  187 us
    all_to_all x2, waiting for transfers between devices, per_device(): lax.all_to_all(states, ('slab', 'gy'), split_axis=0, concat_axis=0, tiled...  35.4 us
    pallas_call x2, Pallas kernels, run_buildings(): pl.pallas_call(functools.partial(building_kernel, COUPLINGS, SUB), grid=(...  33.7 us
    unnamed x18, local copies, waits for them, and re-layouts  8.21 us
    all_to_all x1, starting transfers between devices, per_device(): lax.all_to_all(motion, ('slab', 'gy'), split_axis=0, concat_axis=0, tiled...  6.73 us
    all_to_all x2, starting transfers between devices, per_device(): lax.all_to_all(states, ('slab', 'gy'), split_axis=0, concat_axis=0, tiled...  6.18 us
  transfers between devices with their start and end apart: 3, of which 3 were waited for; matrix products, arithmetic and copies ran while one was open for 1% of the time, Pallas kernels for 5%

profile of v1, /device:TPU:0, one launch (start us, length us, event | category | flops | bytes accessed | tf_op | source)
XLA Modules:
  0.0 307.9 jit_solution(2782993050878474944)
XLA Ops:
  0.6 1.3 convert_reduce_fusion
  1.9 0.7 multiply_add_fusion
  2.6 0.9 select_reduce_fusion
  3.6 0.0 copy-start
  3.6 1.0 copy-done
  4.6 0.0 copy-start.1
  4.6 1.0 copy-done.1
  5.6 0.0 copy-start.2
  5.6 0.9 copy-done.2
  6.5 0.0 copy-start.3
  6.5 0.9 copy-done.3
  7.4 186.6 %shard_map.95 = (f32[3,32,8,128]{3,2,1,0:T(8,128)S(1)}, f32[4,3,8,128]{3,2,1,0:T(8,128)S(1)}) custom-call(f32[3,32,8,128]{3,2,1,0:T(8,128)S(1)} %copy-done, f32[3,32,8,128]{3,2,1,0:T(8,128)S(1)} %copy-done.1, f32[32,8,128]{2,1,0:T(8,128)S(1)} %copy-done.2, f32[32,8,128]{2,1,0:T(8,128)S(1)} %copy-done.3), custom_call_target="tpu_custom_call" | custom-call | tf_op jit(solution)/shard_map/pallas_call | solution.py:231
  194.0 5.6 %all_gather.3 = f32[4,3,8,512]{3,2,1,0:T(8,128)S(1)} all-gather(f32[4,3,8,128]{3,2,1,0:T(8,128)S(1)} %get-tuple-element.5), channel_id=1, replica_groups=mesh['slab'=8,'gy'=4] {'gy'}, dimensions={3}, use_global_device_ids=true | all-gather | bytes 245760 | tf_op jit(solution)/shard_map/all_gather | solution.py:326
  199.6 0.2 copy.30
  199.8 0.6 copy.24
  200.4 5.5 %gather_fusion = f32[2048,12]{1,0:T(8,128)S(1)} fusion(f32[4096,12]{1,0:T(8,128)S(1)} %bitcast.16, s32[2048]{0:T(1024)S(1)} %broadcast_clamp_fusion), kind=kCustom, calls=%fused_computation | custom fusion | bytes 204800 | tf_op jit(solution)/shard_map/jit(_take)/gather | solution.py:328
  205.9 0.4 copy.25
  206.3 0.8 reshape.56
  207.1 6.7 %all-to-all-start = ((f32[32,1,768]{2,1,0:T(1,128)}), f32[32,1,768]{2,1,0:T(1,128)S(1)}, u32[]{:S(2)}, u32[]{:S(2)}) async-start(f32[32,1,768]{2,1,0:T(1,128)} %reshape.56), calls=%async_computation | async-start | bytes 196608 | tf_op jit(solution)/shard_map/all_to_all | solution.py:330
  213.8 1.6 copy.28.f_ref
  215.4 6.2 %all-to-all-done = f32[32,1,768]{2,1,0:T(1,128)S(1)} async-done(((f32[32,1,768]{2,1,0:T(1,128)}), f32[32,1,768]{2,1,0:T(1,128)S(1)}, u32[]{:S(2)}, u32[]{:S(2)}) %all-to-all-start) | async-done | bytes 98336 | tf_op jit(solution)/shard_map/all_to_all | solution.py:330
  221.6 0.5 broadcast.62
  222.1 0.9 reduce
  223.0 0.1 reshape.57
  223.1 0.2 copy.26
  223.3 1.4 copy.27
  224.7 16.9 %shard_map.96 = f32[32,32,256]{2,1,0:T(8,128)} custom-call(f32[32,64,12]{2,1,0:T(8,128)} %bitcast.23, f32[32,3,256]{2,1,0:T(4,128)} %copy.28.f_ref, bf16[32,256,256]{2,1,0:T(8,128)(2,1)} %t_ref.3), custom_call_target="tpu_custom_call" | custom-call | flops 3221225472 | bytes 3145728 | tf_op jit(solution)/shard_map/pallas_call | solution.py:285
  241.5 2.6 all-to-all-start.1
  244.2 0.0 copy-start.5
  244.2 16.9 %shard_map.97 = f32[32,32,256]{2,1,0:T(8,128)} custom-call(f32[32,64,12]{2,1,0:T(8,128)} %bitcast.24, f32[32,3,256]{2,1,0:T(4,128)} %copy.28.f_ref, bf16[32,256,256]{2,1,0:T(8,128)(2,1)} %t_ref.3), custom_call_target="tpu_custom_call" | custom-call | flops 3221225472 | bytes 3145728 | tf_op jit(solution)/shard_map/pallas_call | solution.py:285
  261.1 9.3 %all-to-all-done.1 = f32[32,32,256]{2,1,0:T(8,128)S(1)} async-done(((f32[32,32,256]{2,1,0:T(8,128)}), f32[32,32,256]{2,1,0:T(8,128)S(1)}, u32[]{:S(2)}, u32[]{:S(2)}) %all-to-all-start.1) | async-done | bytes 1048608 | tf_op jit(solution)/shard_map/all_to_all | solution.py:338
  270.4 3.5 %all-to-all-start.2 = ((f32[32,32,256]{2,1,0:T(8,128)}), f32[32,32,256]{2,1,0:T(8,128)S(1)}, u32[]{:S(2)}, u32[]{:S(2)}) async-start(f32[32,32,256]{2,1,0:T(8,128)} %shard_map.97), calls=%async_computation.2 | async-start | bytes 2097152 | tf_op jit(solution)/shard_map/all_to_all | solution.py:338
  273.9 0.0 copy-done.5
  273.9 0.1 add_add_fusion
  274.0 26.1 %all-to-all-done.2 = f32[32,32,256]{2,1,0:T(8,128)S(1)} async-done(((f32[32,32,256]{2,1,0:T(8,128)}), f32[32,32,256]{2,1,0:T(8,128)S(1)}, u32[]{:S(2)}, u32[]{:S(2)}) %all-to-all-start.2) | async-done | bytes 1048608 | tf_op jit(solution)/shard_map/all_to_all | solution.py:338
  300.1 0.0 copy-start.4
  300.1 1.0 copy-done.4
  301.1 1.4 pad_maximum_fusion
  302.5 4.7 %gather_fusion.1 = f32[1024,256]{1,0:T(8,128)} fusion(f32[2048,256]{1,0:T(8,128)S(1)} %pad_maximum_fusion, s32[1024]{0:T(1024)S(1)} %broadcast_clamp_fusion.1), kind=kCustom, calls=%fused_computation.1 | custom fusion | bytes 2101248 | tf_op jit(solution)/shard_map/jit(_take)/gather | solution.py:346
  307.1 0.7 copy.32
  (3 shorter events, 0.0 us)
Async XLA Ops:
  3.6 1.0 copy-start
  4.6 1.0 copy-start.1
  5.6 0.9 copy-start.2
  6.5 0.9 copy-start.3
  207.1 14.5 %all-to-all-start = ((f32[32,1,768]{2,1,0:T(1,128)}), f32[32,1,768]{2,1,0:T(1,128)S(1)}, u32[]{:S(2)}, u32[]{:S(2)}) async-start(f32[32,1,768]{2,1,0:T(1,128)} %reshape.56), calls=%async_computation | async-start | bytes 196608 | tf_op jit(solution)/shard_map/all_to_all | solution.py:330
  241.5 28.8 %all-to-all-start.1 = ((f32[32,32,256]{2,1,0:T(8,128)}), f32[32,32,256]{2,1,0:T(8,128)S(1)}, u32[]{:S(2)}, u32[]{:S(2)}) async-start(f32[32,32,256]{2,1,0:T(8,128)} %shard_map.96), calls=%async_computation.1 | async-start | bytes 2097152 | tf_op jit(solution)/shard_map/all_to_all | solution.py:338
  244.2 29.7 %copy-start.5 = (s32[1024,1]{0,1:T(1,128)S(1)}, s32[1024,1]{0,1:T(1,128)}, u32[]{:S(2)}) copy-start(s32[1024,1]{0,1:T(1,128)} %param.13) | copy-start | bytes 12292
  270.4 29.8 %all-to-all-start.2 = ((f32[32,32,256]{2,1,0:T(8,128)}), f32[32,32,256]{2,1,0:T(8,128)S(1)}, u32[]{:S(2)}, u32[]{:S(2)}) async-start(f32[32,32,256]{2,1,0:T(8,128)} %shard_map.97), calls=%async_computation.2 | async-start | bytes 2097152 | tf_op jit(solution)/shard_map/all_to_all | solution.py:338
  300.1 1.0 copy-start.4

commit v2 on v1

--- a/solution.py
+++ b/solution.py
@@ -30,7 +30,7 @@
 
 def grid_kernel(
     steps, every, d_ref, p_ref, sh_ref, bk_ref, f_ref, surf_ref,
-    buf, ps, pr, ht, ah, hx, e_ref, s_ref, send, recv,
+    buf, ps, pr, ht, ah, hx, e_ref, s_ref, bb_ref, cc_ref, send, recv,
 ):
     nz, cx, cy = sh_ref.shape
     slab, gy = lax.axis_index("slab"), lax.axis_index("gy")
@@ -118,19 +118,35 @@
             buf[par, c, 0, 8:16, :] = buf[par, c, 4, 8:16, :]
             buf[par, c, 1, 8:16, :] = buf[par, c, 3, 8:16, :]
 
-        for k in range(8):
-            @pl.when(exists(*DIRECTIONS[k]))
-            def _():
-                copy_of(k, par).wait_send()
-        for k in range(8):
-            dx, dy = DIRECTIONS[k]
-            @pl.when(exists(-dx, -dy))
-            def _():
-                copy_of(k, par).wait_recv()
-
-        for lo in (0, 16):
-            buf[par, 2, 0, lo : lo + 8, :] = buf[par, 2, 4, lo : lo + 8, :]
-            buf[par, 2, 1, lo : lo + 8, :] = buf[par, 2, 3, lo : lo + 8, :]
+        def u(c, d, shift, lo):
+            return buf[par, c, pl.ds(d + 2 + shift, PLANES), lo : lo + 8, :]
+
+        def core(c, d):
+            return (new, c, pl.ds(d + 2, PLANES), slice(8, 16), slice(None))
+
+        def local(b, carry):
+            d = b * PLANES
+            sh = sh_ref[pl.ds(d, PLANES)]
+            bk = bk_ref[pl.ds(d, PLANES)]
+            for c in range(3):
+                mid = u(c, d, 0, 8)
+                near = (u(c, d, 1, 8), u(c, d, -1, 8), u(c, d, 2, 8), u(c, d, -2, 8))
+                coef = sh + bk if c == 2 else sh
+                buf[core(c, d)] = 2.0 * mid - buf[core(c, d)] + coef * second(mid, *near)
+                if c == 2:
+                    cc_ref[pl.ds(d, PLANES)] = first(*near)
+            return carry
+
+        lax.fori_loop(0, blocks, local, 0)
+
+        def await_halos(ks):
+            for k in ks:
+                dx, dy = DIRECTIONS[k]
+                @pl.when(exists(-dx, -dy))
+                def _():
+                    copy_of(k, par).wait_recv()
+
+        await_halos(range(2, 8))
 
         from_left = lax.rem(lane, 4) < 2
 
@@ -155,15 +171,32 @@
         ht[2, 0] = ht[2, 4]
         ht[2, 1] = ht[2, 3]
 
-        def u(c, d, shift, lo):
-            return buf[par, c, pl.ds(d + 2 + shift, PLANES), lo : lo + 8, :]
+        def sideways(b, carry):
+            d = b * PLANES
+            sh = sh_ref[pl.ds(d, PLANES)]
+            bk = bk_ref[pl.ds(d, PLANES)]
+            for c in range(3):
+                mid = u(c, d, 0, 8)
+                near = along_y(mid, ht[c, pl.ds(d + 2, PLANES)])
+                coef = sh + bk if c == 1 else sh
+                buf[core(c, d)] = buf[core(c, d)] + coef * second(mid, *near)
+                if c == 1:
+                    bb_ref[pl.ds(d, PLANES)] = first(*near)
+            return carry
+
+        lax.fori_loop(0, blocks, sideways, 0)
+
+        await_halos(range(2))
+        for lo in (0, 16):
+            buf[par, 2, 0, lo : lo + 8, :] = buf[par, 2, 4, lo : lo + 8, :]
+            buf[par, 2, 1, lo : lo + 8, :] = buf[par, 2, 3, lo : lo + 8, :]
 
         def prepare(b, carry):
             d = b * PLANES
             a = first(u(0, d, 0, 9), u(0, d, 0, 7), u(0, d, 0, 10), u(0, d, 0, 6))
-            bb = first(*along_y(u(1, d, 0, 8), ht[1, pl.ds(d + 2, PLANES)]))
+            bb = bb_ref[pl.ds(d, PLANES)]
             e_ref[pl.ds(d + 2, PLANES)] = a + bb
-            cc = first(u(2, d, 1, 8), u(2, d, -1, 8), u(2, d, 2, 8), u(2, d, -2, 8))
+            cc = cc_ref[pl.ds(d, PLANES)]
             s_ref[pl.ds(d, PLANES), 8:16, :] = bb + cc
 
             def mixed(comp, shift):
@@ -195,28 +228,27 @@
                 return e_ref[pl.ds(d + 2 + shift, PLANES)]
 
             a = first(u(0, d, 0, 9), u(0, d, 0, 7), u(0, d, 0, 10), u(0, d, 0, 6))
-            cc = first(u(2, d, 1, 8), u(2, d, -1, 8), u(2, d, 2, 8), u(2, d, -2, 8))
+            cc = cc_ref[pl.ds(d, PLANES)]
             c_halo = first(h(2, 1), h(2, -1), h(2, 2), h(2, -2))
             t_halo = ah[pl.ds(d, PLANES)] + c_halo
             for c in range(3):
                 mid = u(c, d, 0, 8)
-                along = (
-                    second(mid, u(c, d, 0, 9), u(c, d, 0, 7), u(c, d, 0, 10), u(c, d, 0, 6)),
-                    second(mid, *along_y(mid, h(c, 0))),
-                    second(mid, u(c, d, 1, 8), u(c, d, -1, 8), u(c, d, 2, 8), u(c, d, -2, 8)),
-                )
+                along = second(mid, u(c, d, 0, 9), u(c, d, 0, 7), u(c, d, 0, 10), u(c, d, 0, 6))
                 if c == 0:
                     cross = first(s(9), s(7), s(10), s(6))
                 elif c == 1:
                     cross = first(*along_y(a + cc, t_halo))
                 else:
                     cross = first(e(1), e(-1), e(2), e(-2))
-                acc = sh * (along[0] + along[1] + along[2]) + bk * (along[c] + cross)
-                place = (new, c, pl.ds(d + 2, PLANES), slice(8, 16), slice(None))
-                buf[place] = 2.0 * mid - buf[place] + acc
+                coef = sh + bk if c == 0 else sh
+                buf[core(c, d)] = buf[core(c, d)] + (coef * along + bk * cross)
             return carry
 
         lax.fori_loop(0, blocks, advance, 0)
+        for k in range(8):
+            @pl.when(exists(*DIRECTIONS[k]))
+            def _():
+                copy_of(k, par).wait_send()
         surf_ref[lax.div(n, every)] = buf[new, :, 2, 8:16, :]
         return carry
 
@@ -245,6 +277,8 @@
             pltpu.VMEM((nz, cx, cy), f32),
             pltpu.VMEM((nz + 4, cx, cy), f32),
             pltpu.VMEM((nz, cx + 16, cy), f32),
+            pltpu.VMEM((nz, cx, cy), f32),
+            pltpu.VMEM((nz, cx, cy), f32),
             pltpu.SemaphoreType.DMA((2, 8)),
             pltpu.SemaphoreType.DMA((2, 8)),
         ],

time: 309 us -> 322 us (1.042)
  Pallas kernels: 220 us -> 233 us
    pallas_call x1, Pallas kernels: 187 us -> 200 us  [run_grid(): pl.pallas_call(functools.partial(grid_kernel, COUPLINGS * EVERY, EVERY),...]
where the time goes in v2:
time: 322 us; the launch traced here: 321 us
  Pallas kernels  233 us (72%)
  waiting for transfers between devices  41.6 us (13%)
  local copies, waits for them, and re-layouts  21.5 us (7%)
  starting transfers between devices  13.2 us (4%)
  blocking collectives  5.6 us (2%)
  other arithmetic  5.23 us (2%)
    pallas_call x1, Pallas kernels, run_grid(): pl.pallas_call(functools.partial(grid_kernel, COUPLINGS * EVERY, EVERY),...  200 us
    all_to_all x2, waiting for transfers between devices, per_device(): lax.all_to_all(states, ('slab', 'gy'), split_axis=0, concat_axis=0, tiled...  35.4 us
    pallas_call x2, Pallas kernels, run_buildings(): pl.pallas_call(functools.partial(building_kernel, COUPLINGS, SUB), grid=(...  33.7 us
    unnamed x18, local copies, waits for them, and re-layouts  8.21 us
    all_to_all x1, starting transfers between devices, per_device(): lax.all_to_all(motion, ('slab', 'gy'), split_axis=0, concat_axis=0, tiled...  6.97 us
  transfers between devices with their start and end apart: 3, of which 3 were waited for; matrix products, arithmetic and copies ran while one was open for 1% of the time, Pallas kernels for 5%

profile of v2, /device:TPU:0, one launch (start us, length us, event | category | flops | bytes accessed | tf_op | source)
XLA Modules:
  0.0 321.1 jit_solution(18210578106469505677)
XLA Ops:
  0.6 1.3 convert_reduce_fusion
  1.9 0.7 multiply_add_fusion
  2.6 0.9 select_reduce_fusion
  3.6 0.0 copy-start
  3.6 1.0 copy-done
  4.6 0.0 copy-start.1
  4.6 1.0 copy-done.1
  5.6 0.0 copy-start.2
  5.6 0.9 copy-done.2
  6.5 0.0 copy-start.3
  6.5 0.9 copy-done.3
  7.4 199.6 %shard_map.95 = (f32[3,32,8,128]{3,2,1,0:T(8,128)S(1)}, f32[4,3,8,128]{3,2,1,0:T(8,128)S(1)}) custom-call(f32[3,32,8,128]{3,2,1,0:T(8,128)S(1)} %copy-done, f32[3,32,8,128]{3,2,1,0:T(8,128)S(1)} %copy-done.1, f32[32,8,128]{2,1,0:T(8,128)S(1)} %copy-done.2, f32[32,8,128]{2,1,0:T(8,128)S(1)} %copy-done.3), custom_call_target="tpu_custom_call" | custom-call | tf_op jit(solution)/shard_map/pallas_call | solution.py:263
  207.0 5.6 %all_gather.3 = f32[4,3,8,512]{3,2,1,0:T(8,128)S(1)} all-gather(f32[4,3,8,128]{3,2,1,0:T(8,128)S(1)} %get-tuple-element.5), channel_id=1, replica_groups=mesh['slab'=8,'gy'=4] {'gy'}, dimensions={3}, use_global_device_ids=true | all-gather | bytes 245760 | tf_op jit(solution)/shard_map/all_gather | solution.py:360
  212.6 0.2 copy.30
  212.8 0.6 copy.24
  213.4 5.5 %gather_fusion = f32[2048,12]{1,0:T(8,128)S(1)} fusion(f32[4096,12]{1,0:T(8,128)S(1)} %bitcast.16, s32[2048]{0:T(1024)S(1)} %broadcast_clamp_fusion), kind=kCustom, calls=%fused_computation | custom fusion | bytes 204800 | tf_op jit(solution)/shard_map/jit(_take)/gather | solution.py:362
  218.9 0.4 copy.25
  219.3 0.8 reshape.56
  220.1 7.0 %all-to-all-start = ((f32[32,1,768]{2,1,0:T(1,128)}), f32[32,1,768]{2,1,0:T(1,128)S(1)}, u32[]{:S(2)}, u32[]{:S(2)}) async-start(f32[32,1,768]{2,1,0:T(1,128)} %reshape.56), calls=%async_computation | async-start | bytes 196608 | tf_op jit(solution)/shard_map/all_to_all | solution.py:364
  227.1 1.6 copy.28.f_ref
  228.7 6.2 %all-to-all-done = f32[32,1,768]{2,1,0:T(1,128)S(1)} async-done(((f32[32,1,768]{2,1,0:T(1,128)}), f32[32,1,768]{2,1,0:T(1,128)S(1)}, u32[]{:S(2)}, u32[]{:S(2)}) %all-to-all-start) | async-done | bytes 98336 | tf_op jit(solution)/shard_map/all_to_all | solution.py:364
  234.8 0.5 broadcast.62
  235.4 0.9 reduce
  236.2 0.1 reshape.57
  236.3 0.2 copy.26
  236.5 1.4 copy.27
  237.9 16.9 %shard_map.96 = f32[32,32,256]{2,1,0:T(8,128)} custom-call(f32[32,64,12]{2,1,0:T(8,128)} %bitcast.23, f32[32,3,256]{2,1,0:T(4,128)} %copy.28.f_ref, bf16[32,256,256]{2,1,0:T(8,128)(2,1)} %t_ref.3), custom_call_target="tpu_custom_call" | custom-call | flops 3221225472 | bytes 3145728 | tf_op jit(solution)/shard_map/pallas_call | solution.py:319
  254.8 2.6 all-to-all-start.1
  257.4 0.0 copy-start.5
  257.4 16.9 %shard_map.97 = f32[32,32,256]{2,1,0:T(8,128)} custom-call(f32[32,64,12]{2,1,0:T(8,128)} %bitcast.24, f32[32,3,256]{2,1,0:T(4,128)} %copy.28.f_ref, bf16[32,256,256]{2,1,0:T(8,128)(2,1)} %t_ref.3), custom_call_target="tpu_custom_call" | custom-call | flops 3221225472 | bytes 3145728 | tf_op jit(solution)/shard_map/pallas_call | solution.py:319
  274.3 9.3 %all-to-all-done.1 = f32[32,32,256]{2,1,0:T(8,128)S(1)} async-done(((f32[32,32,256]{2,1,0:T(8,128)}), f32[32,32,256]{2,1,0:T(8,128)S(1)}, u32[]{:S(2)}, u32[]{:S(2)}) %all-to-all-start.1) | async-done | bytes 1048608 | tf_op jit(solution)/shard_map/all_to_all | solution.py:372
  283.6 3.5 %all-to-all-start.2 = ((f32[32,32,256]{2,1,0:T(8,128)}), f32[32,32,256]{2,1,0:T(8,128)S(1)}, u32[]{:S(2)}, u32[]{:S(2)}) async-start(f32[32,32,256]{2,1,0:T(8,128)} %shard_map.97), calls=%async_computation.2 | async-start | bytes 2097152 | tf_op jit(solution)/shard_map/all_to_all | solution.py:372
  287.2 0.0 copy-done.5
  287.2 0.1 add_add_fusion
  287.2 26.1 %all-to-all-done.2 = f32[32,32,256]{2,1,0:T(8,128)S(1)} async-done(((f32[32,32,256]{2,1,0:T(8,128)}), f32[32,32,256]{2,1,0:T(8,128)S(1)}, u32[]{:S(2)}, u32[]{:S(2)}) %all-to-all-start.2) | async-done | bytes 1048608 | tf_op jit(solution)/shard_map/all_to_all | solution.py:372
  313.4 0.0 copy-start.4
  313.4 1.0 copy-done.4
  314.3 1.4 pad_maximum_fusion
  315.7 4.7 %gather_fusion.1 = f32[1024,256]{1,0:T(8,128)} fusion(f32[2048,256]{1,0:T(8,128)S(1)} %pad_maximum_fusion, s32[1024]{0:T(1024)S(1)} %broadcast_clamp_fusion.1), kind=kCustom, calls=%fused_computation.1 | custom fusion | bytes 2101248 | tf_op jit(solution)/shard_map/jit(_take)/gather | solution.py:380
  320.4 0.7 copy.32
  (3 shorter events, 0.0 us)
Async XLA Ops:
  3.6 1.0 copy-start
  4.6 1.0 copy-start.1
  5.6 0.9 copy-start.2
  6.5 0.9 copy-start.3
  220.1 14.8 %all-to-all-start = ((f32[32,1,768]{2,1,0:T(1,128)}), f32[32,1,768]{2,1,0:T(1,128)S(1)}, u32[]{:S(2)}, u32[]{:S(2)}) async-start(f32[32,1,768]{2,1,0:T(1,128)} %reshape.56), calls=%async_computation | async-start | bytes 196608 | tf_op jit(solution)/shard_map/all_to_all | solution.py:364
  254.8 28.8 %all-to-all-start.1 = ((f32[32,32,256]{2,1,0:T(8,128)}), f32[32,32,256]{2,1,0:T(8,128)S(1)}, u32[]{:S(2)}, u32[]{:S(2)}) async-start(f32[32,32,256]{2,1,0:T(8,128)} %shard_map.96), calls=%async_computation.1 | async-start | bytes 2097152 | tf_op jit(solution)/shard_map/all_to_all | solution.py:372
  257.4 29.7 %copy-start.5 = (s32[1024,1]{0,1:T(1,128)S(1)}, s32[1024,1]{0,1:T(1,128)}, u32[]{:S(2)}) copy-start(s32[1024,1]{0,1:T(1,128)} %param.13) | copy-start | bytes 12292
  283.6 29.8 %all-to-all-start.2 = ((f32[32,32,256]{2,1,0:T(8,128)}), f32[32,32,256]{2,1,0:T(8,128)S(1)}, u32[]{:S(2)}, u32[]{:S(2)}) async-start(f32[32,32,256]{2,1,0:T(8,128)} %shard_map.97), calls=%async_computation.2 | async-start | bytes 2097152 | tf_op jit(solution)/shard_map/all_to_all | solution.py:372
  313.4 1.0 copy-start.4
